TPU v7x, 32 devices: a whole 2x2x4 slice. The times are simulated.
32 devices in a mesh: chan: 16 (over z, y, core), tm: 2 (over x).
Axes of the slice: x: 2, y: 2, z: 4, core: 2. Of those that a mesh axis runs over, the one named last changes fastest.
Arguments:
- voltages: bfloat16 [2, 512, 256, 512], P(None, None, 'chan', 'tm'), may hold values from -6 to 6, as said below
- flag_mask: int32 [4, 256], P('tm', 'chan'), may hold values from 0 to 1, as said below
- flagged_prefix_counts: int32 [4, 256], P('tm', 'chan'), may hold values from 0 to 127
Outputs:
- visibilities: float32 [512, 2, 256, 256], P(('chan', 'tm'))
Inputs may be any that keep to these rules, and one draw needn't show every extreme that they name: `voltages`: samples that keep drops count as zero; a program may move only the kept samples, in any compact form. `flag_mask`: 1 keeps the block of 128 samples of an antenna, 0 drops it; some antennas are dropped in every block. The first flagged_prefix_counts samples of a kept block are flagged; flags and counts may be packed several to a word wherever they are moved.
All inputs are finite; a program needn't handle non-finite values.
Results may differ from a plain program's by a relative error of at most 0.0003.
Values may be sent and summed in bfloat16 or wider, within the bound.
A program may use at most 128 MiB of HBM per device.

v0:
```python
import functools

import jax
import jax.numpy as jnp
from jax import lax
from jax.experimental import pallas as pl
from jax.experimental.pallas import tpu as pltpu
from jax.sharding import PartitionSpec as P

FLAG_BLOCK_WIDTH = 128
LANES = 128
MESH = pl.DeviceIdType.MESH
NT = (((1,), (1,)), ((), ()))


def exchange_kernel(
    n_chan, n_tm, groups, volt_ref, limit_ref, out_ref,
    held, table, cols, keep, inverse, send_sem, recv_sem, table_send, table_recv,
):
    n = n_chan * n_tm
    channels = held.shape[1]
    step = channels // groups
    antennas, samples = volt_ref.shape[2], volt_ref.shape[3]
    total_antennas = n_chan * antennas
    local_blocks = samples // FLAG_BLOCK_WIDTH
    my_chan, my_tm = lax.axis_index("chan"), lax.axis_index("tm")
    me = my_chan * n_tm + my_tm

    def swing(m):
        return (m + 1) // 2 * (1 - 2 * lax.rem(m + 1, 2))

    def hop(k):
        return n // 2 + swing(k - 1)

    def place(k):
        other = lax.rem(me + hop(k), n)
        return other, (other // n_tm, lax.rem(other, n_tm))

    barrier = pltpu.get_barrier_semaphore()

    def greet(k, carry):
        pl.semaphore_signal(barrier, inc=1, device_id=place(k)[1], device_id_type=MESH)
        return carry

    lax.fori_loop(1, n, greet, 0)
    pl.semaphore_wait(barrier, n - 1)

    def landing(g):
        return held.at[
            :, pl.ds(g * step, step), my_chan, :, pl.ds(pl.multiple_of(my_tm * samples, LANES), samples)
        ]

    def flag_copy(k):
        return pltpu.make_async_remote_copy(
            src_ref=limit_ref, dst_ref=table.at[me], send_sem=table_send.at[k], recv_sem=table_recv,
            device_id=place(k)[1], device_id_type=MESH,
        )

    def volt_copy(g, k):
        other, where = place(k)
        return pltpu.make_async_remote_copy(
            src_ref=volt_ref.at[:, pl.ds(other * channels + g * step, step)],
            dst_ref=landing(g), send_sem=send_sem.at[g, k], recv_sem=recv_sem.at[g],
            device_id=where, device_id_type=MESH,
        )

    def each(body):
        def run(k, carry):
            body(k)
            return carry

        lax.fori_loop(1, n, run, 0)

    each(lambda k: flag_copy(k).start())
    for g in range(groups):
        each(lambda k, g=g: volt_copy(g, k).start())
    pltpu.make_async_copy(limit_ref, table.at[me], table_recv).start()
    for g in range(groups):
        pltpu.make_async_copy(
            volt_ref.at[:, pl.ds(me * channels + g * step, step)], landing(g), recv_sem.at[g]
        ).start()

    pltpu.make_async_copy(table, table, table_recv).wait()
    rows = table[:, 0, :].astype(jnp.float32)
    padding = -n % LANES
    if padding:
        rows = jnp.concatenate([rows, jnp.zeros((padding, rows.shape[1]), jnp.float32)], axis=0)
    turned = rows.T
    lane = lax.broadcasted_iota(jnp.int32, (total_antennas, LANES), 1).astype(jnp.float32)
    pairs = jnp.zeros((total_antennas, total_antennas), jnp.float32)
    for t in range(n_tm):
        for b in range(local_blocks):
            q = t * local_blocks + b
            for c in range(n_chan):
                source = c * n_tm + t
                cols[c * antennas:(c + 1) * antennas, :] = jnp.broadcast_to(
                    turned[b * antennas:(b + 1) * antennas, source:source + 1], (antennas, LANES)
                )
            column = cols[...]
            keep[:, q * LANES:(q + 1) * LANES] = jnp.where(lane >= column, 1.0, 0.0).astype(keep.dtype)
            pairs += FLAG_BLOCK_WIDTH - jnp.maximum(column[:, :1], column.T[:1, :])
    inverse[...] = 1.0 / jnp.maximum(pairs, 1.0)

    def correlate(c, carry):
        size = (total_antennas, keep.shape[1])
        real = held[0, c].reshape(size) * keep[...]
        imag = held[1, c].reshape(size) * keep[...]
        same = lax.dot_general(real, real, NT, preferred_element_type=jnp.float32)
        same += lax.dot_general(imag, imag, NT, preferred_element_type=jnp.float32)
        cross = lax.dot_general(imag, real, NT, preferred_element_type=jnp.float32)
        out_ref[c, 0] = same * inverse[...]
        out_ref[c, 1] = (cross - cross.T) * inverse[...]
        return carry

    for g in range(groups):
        part = held.at[:, pl.ds(g * step, step)]
        pltpu.make_async_copy(part, part, recv_sem.at[g]).wait()
        lax.fori_loop(g * step, (g + 1) * step, correlate, 0)

    each(lambda k: flag_copy(k).wait_send())
    for g in range(groups):
        each(lambda k, g=g: volt_copy(g, k).wait_send())


def shards(n_chan, n_tm, voltages, flag_mask, flagged_prefix_counts):
    parts, all_channels, antennas, samples = voltages.shape
    n = n_chan * n_tm
    channels = all_channels // n
    total_antennas, total_samples = antennas * n_chan, samples * n_tm
    groups = max(g for g in (4, 2, 1) if channels % g == 0)
    limits = jnp.where(flag_mask == 1, flagged_prefix_counts, FLAG_BLOCK_WIDTH).reshape(1, -1)
    limits = jnp.pad(limits, ((0, 0), (0, -limits.shape[1] % LANES)))
    width = limits.shape[1]
    return pl.pallas_call(
        functools.partial(exchange_kernel, n_chan, n_tm, groups),
        out_shape=pltpu.VMEM((channels, 2, total_antennas, total_antennas), jnp.float32),
        in_specs=[pl.BlockSpec(memory_space=pl.ANY), pl.BlockSpec(memory_space=pltpu.VMEM)],
        out_specs=pl.BlockSpec(memory_space=pltpu.VMEM),
        scratch_shapes=[
            pltpu.VMEM((parts, channels, n_chan, antennas, total_samples), voltages.dtype),
            pltpu.VMEM((n, 1, width), jnp.int32),
            pltpu.VMEM((total_antennas, LANES), jnp.float32),
            pltpu.VMEM((total_antennas, total_samples), voltages.dtype),
            pltpu.VMEM((total_antennas, total_antennas), jnp.float32),
            pltpu.SemaphoreType.DMA((groups, n)),
            pltpu.SemaphoreType.DMA((groups,)),
            pltpu.SemaphoreType.DMA((n,)),
            pltpu.SemaphoreType.DMA,
        ],
        compiler_params=pltpu.CompilerParams(
            collective_id=0, has_side_effects=True, vmem_limit_bytes=48 * 1024 * 1024
        ),
    )(voltages, limits)


def solution(mesh):
    placed = (P(None, None, "chan", "tm"), P("tm", "chan"), P("tm", "chan"))
    return jax.shard_map(
        functools.partial(shards, mesh.shape["chan"], mesh.shape["tm"]),
        mesh=mesh,
        in_specs=placed,
        out_specs=P(("chan", "tm"), None, None, None),
        check_vma=False,
    )
```

profile of v0, /device:TPU:0, one launch (start us, length us, event | category | flops | bytes accessed | tf_op | source)
XLA Modules:
  0.0 197.9 jit_solution(15271741057301542128)
XLA Ops:
  0.0 0.7 compare_select_fusion
  0.7 0.1 reshape.3
  0.8 0.5 pad.4.limit_ref
  1.3 193.2 %shard_map.37 = f32[16,2,256,256]{3,2,1,0:T(8,128)S(1)} custom-call(bf16[2,512,16,256]{3,2,1,0:T(8,128)(2,1)} %volt_ref.1, s32[1,128]{1,0:T(1,128)} %pad.4.limit_ref), custom_call_target="tpu_custom_call" | custom-call | tf_op jit(solution)/shard_map/pallas_call | solution.py:134
  194.5 3.4 %copy.5 = f32[16,2,256,256]{3,2,1,0:T(8,128)} copy(f32[16,2,256,256]{3,2,1,0:T(8,128)S(1)} %shard_map.37) | data formatting | bytes 16777216
where the time goes:
time: 198 us
  Pallas kernels  193 us (97%)
  local copies, waits for them, and re-layouts  4 us (2%)
    pallas_call x1, Pallas kernels, shards(): pl.pallas_call(functools.partial(exchange_kernel, n_chan, n_tm, groups),...  193 us

commit v1 on v0

--- a/solution.py
+++ b/solution.py
@@ -9,6 +9,7 @@
 
 FLAG_BLOCK_WIDTH = 128
 LANES = 128
+SUBLANES = 8
 MESH = pl.DeviceIdType.MESH
 NT = (((1,), (1,)), ((), ()))
 
@@ -153,10 +154,385 @@
     )(voltages, limits)
 
 
+def rotate(x, shift):
+    return pltpu.roll(x, shift, axis=1)
+
+
+def pack_kernel(
+    n_chan, n_tm, levels, volt_ref, mask_ref, count_ref, both_ref, table_ref, meta_ref, level_ref,
+    held, theirs, mine, row, table, steps,
+    load_sem, flag_send, flag_recv, pair_send, pair_recv, keep_sem, own_sem,
+):
+    n = n_chan * n_tm
+    parts, all_channels, antennas, samples = volt_ref.shape
+    channels = all_channels // n
+    chips, groups, entries = mine.shape[0], mine.shape[1], mine.shape[2]
+    width = SUBLANES // parts
+    blocks = samples // FLAG_BLOCK_WIDTH
+    segments = blocks * antennas
+    my_chan, my_tm = lax.axis_index("chan"), lax.axis_index("tm")
+    me = my_chan * n_tm + my_tm
+    side = lax.rem(my_chan, 2)
+    partner = (my_chan + 1 - 2 * side, my_tm)
+
+    def place(k):
+        other = lax.rem(me + k, n)
+        return (other // n_tm, lax.rem(other, n_tm))
+
+    barrier = pltpu.get_barrier_semaphore()
+
+    def greet(k, carry):
+        pl.semaphore_signal(barrier, inc=1, device_id=place(k), device_id_type=MESH)
+        return carry
+
+    lax.fori_loop(1, n, greet, 0)
+
+    def load(d):
+        part = pl.ds(d * channels, channels)
+        return pltpu.make_async_copy(volt_ref.at[:, part], held.at[:, part], load_sem.at[d])
+
+    def device_of(m, which):
+        chan = m // n_tm * 2 + lax.rem(side + which, 2)
+        return chan * n_tm + lax.rem(m, n_tm)
+
+    def start_load(m, carry):
+        load(device_of(m, 1)).start()
+        load(device_of(m, 0)).start()
+        return carry
+
+    lax.fori_loop(0, chips, start_load, 0)
+
+    lane = lax.broadcasted_iota(jnp.int32, (SUBLANES, LANES), 1)
+    limits = jnp.full((SUBLANES, LANES), FLAG_BLOCK_WIDTH, jnp.int32)
+    start = jnp.int32(0)
+    for s in range(segments):
+        b, i = s // antennas, s % antennas
+        limit = jnp.where(mask_ref[b, i] == 1, count_ref[b, i], FLAG_BLOCK_WIDTH)
+        limits = jnp.where(lane == s, limit, limits)
+        first = start & (LANES - 1)
+        spills = first + FLAG_BLOCK_WIDTH - limit > LANES
+        steps[0, s] = (first - limit) & (LANES - 1)
+        steps[1, s] = first
+        steps[2, s] = jnp.where(spills, 0, first)
+        start = start + FLAG_BLOCK_WIDTH - limit
+    row[...] = limits[:1]
+
+    old = lax.broadcasted_iota(jnp.int32, (SUBLANES * antennas, SUBLANES * antennas), 1)
+    new = lax.broadcasted_iota(jnp.int32, (SUBLANES * antennas, SUBLANES * antennas), 0)
+    turn = jnp.where(old == lax.rem(new, SUBLANES) * antennas + new // SUBLANES, 1.0, 0.0).astype(volt_ref.dtype)
+
+    def pack(d, m, target):
+        for g in range(groups):
+            part = held[:, pl.ds(d * channels + g * width, width)].reshape(SUBLANES * antennas, samples)
+            flat = jnp.dot(turn, part, preferred_element_type=jnp.float32)
+            carry = jnp.zeros((SUBLANES, LANES), jnp.float32)
+            for s in range(segments):
+                b, i = s // antennas, s % antennas
+                piece = flat[i * SUBLANES:(i + 1) * SUBLANES, b * LANES:(b + 1) * LANES]
+                piece = rotate(piece, steps[0, s])
+                target[m, g, s] = jnp.where(lane >= steps[1, s], piece, carry).astype(target.dtype)
+                carry = jnp.where(lane >= steps[2, s], piece, carry)
+            target[m, g, segments] = carry.astype(target.dtype)
+
+    pl.semaphore_wait(barrier, n - 1)
+
+    def flag_copy(k):
+        return pltpu.make_async_remote_copy(
+            src_ref=row, dst_ref=table.at[me], send_sem=flag_send.at[k], recv_sem=flag_recv,
+            device_id=place(k), device_id_type=MESH,
+        )
+
+    def send_flags(k, carry):
+        flag_copy(k).start()
+        return carry
+
+    lax.fori_loop(1, n, send_flags, 0)
+    pltpu.make_async_copy(row, table.at[me], flag_recv).start()
+
+    def pair_copy(m):
+        return pltpu.make_async_remote_copy(
+            src_ref=theirs.at[m], dst_ref=both_ref.at[1, m], send_sem=pair_send.at[m], recv_sem=pair_recv,
+            device_id=partner, device_id_type=MESH,
+        )
+
+    def keep_copy(m):
+        return pltpu.make_async_copy(mine.at[m], both_ref.at[0, m], keep_sem.at[m])
+
+    def chip(m, carry):
+        d = device_of(m, 1)
+        load(d).wait()
+        pack(d, m, theirs)
+        pair_copy(m).start()
+        d = device_of(m, 0)
+        load(d).wait()
+        pack(d, m, mine)
+        keep_copy(m).start()
+        return carry
+
+    lax.fori_loop(0, chips, chip, 0)
+
+    pltpu.make_async_copy(table, table, flag_recv).wait()
+    rows = table[:, 0, :]
+    lanes = lax.broadcasted_iota(jnp.int32, (n, LANES), 1)
+    kept = (FLAG_BLOCK_WIDTH - rows).astype(jnp.float32).astype(jnp.bfloat16)
+    above = jnp.where(
+        lax.broadcasted_iota(jnp.int32, (LANES, LANES), 0) < lax.broadcasted_iota(jnp.int32, (LANES, LANES), 1), 1.0, 0.0
+    ).astype(jnp.bfloat16)
+    offset = jnp.dot(kept, above, preferred_element_type=jnp.float32).astype(jnp.int32)
+    full = jnp.max((offset + (LANES - 1)) >> 7, axis=1, keepdims=True)
+    full = jnp.broadcast_to(full, (n, LANES))
+    to = lax.broadcasted_iota(jnp.int32, (n, n), 0)
+    frm = lax.broadcasted_iota(jnp.int32, (n, n), 1)
+    behind = jnp.where((frm == to - n_tm) & (lax.rem(to // n_tm, 2) == 1), 1.0, 0.0).astype(jnp.bfloat16)
+    base = jnp.dot(behind, full.astype(jnp.float32).astype(jnp.bfloat16), preferred_element_type=jnp.float32).astype(jnp.int32)
+    at = offset >> 7
+    meta_ref[0] = ((base + at) << 16) | ((offset & (LANES - 1)) << 8) | rows
+    place_of = jnp.full((n, LANES), -1, jnp.int32)
+    for s in range(segments + 1):
+        place_of += jnp.where(at[:, s:s + 1] <= lanes, 1, 0)
+    meta_ref[1] = jnp.where(lanes == LANES - 1, full, place_of)
+    table_ref[...] = rows
+    need = jnp.max(base + full, axis=0, keepdims=True)
+    level = jnp.zeros((1, LANES), jnp.int32)
+    for q in levels[:-1]:
+        level += jnp.where(need > q, 1, 0)
+    level_ref[...] = level
+
+    def drain(m, carry):
+        pair_copy(m).wait_send()
+        keep_copy(m).wait()
+        return carry
+
+    lax.fori_loop(0, chips, drain, 0)
+    pltpu.make_async_copy(both_ref.at[1], both_ref.at[1], pair_recv).wait()
+
+    def drain_flags(k, carry):
+        flag_copy(k).wait_send()
+        return carry
+
+    lax.fori_loop(1, n, drain_flags, 0)
+
+
+def unite_kernel(n_chan, n_tm, antennas, samples, sent, both_ref, table_ref, meta_ref, out_ref, *scratch):
+    groups = both_ref.shape[2]
+    landing = scratch[:groups]
+    both, ready, square, cols, inverse, both_sem, send_sem, recv_sem = scratch[groups:]
+    n, chips = n_chan * n_tm, both_ref.shape[1]
+    total_antennas, total_samples = square.shape[1], square.shape[2]
+    blocks = samples // FLAG_BLOCK_WIDTH
+    width = out_ref.shape[0] // groups
+    my_chan, my_tm = lax.axis_index("chan"), lax.axis_index("tm")
+    side = lax.rem(my_chan, 2)
+    here = my_chan // 2 * n_tm + my_tm
+
+    def swing(m):
+        return (m + 1) // 2 * (1 - 2 * lax.rem(m + 1, 2))
+
+    def place(k):
+        other = lax.rem(here + chips // 2 + swing(k - 1), chips)
+        return other, (other // n_tm * 2 + side, lax.rem(other, n_tm))
+
+    barrier = pltpu.get_barrier_semaphore()
+
+    def greet(k, carry):
+        pl.semaphore_signal(barrier, inc=1, device_id=place(k)[1], device_id_type=MESH)
+        return carry
+
+    lax.fori_loop(1, chips, greet, 0)
+    fetch = pltpu.make_async_copy(both_ref, both, both_sem)
+    fetch.start()
+    first_device = (my_chan - side) * n_tm + my_tm
+    split = meta_ref[1, first_device, LANES - 1]
+    fetch.wait()
+
+    def gather(g):
+        def pick(r, carry):
+            second = jnp.where(r < split, 0, 1)
+            entry = meta_ref[1, first_device + second * n_tm, r - second * split]
+            ready[g, :, r] = both[jnp.where(second == side, 0, 1), :, g, entry]
+            return carry
+
+        lax.fori_loop(0, sent, pick, 0)
+
+    def copy(g, k):
+        other, where = place(k)
+        return pltpu.make_async_remote_copy(
+            src_ref=ready.at[g, other], dst_ref=landing[g].at[here, pl.ds(0, sent)],
+            send_sem=send_sem.at[g, k], recv_sem=recv_sem.at[g], device_id=where, device_id_type=MESH,
+        )
+
+    def each(body):
+        def run(k, carry):
+            body(k)
+            return carry
+
+        lax.fori_loop(1, chips, run, 0)
+
+    for g in range(groups):
+        gather(g)
+        if g == 0:
+            pl.semaphore_wait(barrier, chips - 1)
+        each(lambda k, g=g: copy(g, k).start())
+        pltpu.make_async_copy(ready.at[g, here], landing[g].at[here, pl.ds(0, sent)], recv_sem.at[g]).start()
+
+    rows = table_ref[...].astype(jnp.float32)
+    padding = -n % LANES
+    if padding:
+        rows = jnp.concatenate([rows, jnp.zeros((padding, rows.shape[1]), jnp.float32)], axis=0)
+    turned = rows.T
+    pairs = jnp.zeros((total_antennas, total_antennas), jnp.float32)
+    for t in range(n_tm):
+        for b in range(blocks):
+            for c in range(n_chan):
+                source = c * n_tm + t
+                cols[c * antennas:(c + 1) * antennas, :] = jnp.broadcast_to(
+                    turned[b * antennas:(b + 1) * antennas, source:source + 1], (antennas, LANES)
+                )
+            column = cols[...]
+            pairs += FLAG_BLOCK_WIDTH - jnp.maximum(column[:, :1], column.T[:1, :])
+    inverse[...] = 1.0 / jnp.maximum(pairs, 1.0)
+
+    lane = lax.broadcasted_iota(jnp.int32, (SUBLANES, LANES), 1)
+    old = lax.broadcasted_iota(jnp.int32, (SUBLANES * antennas, SUBLANES * antennas), 1)
+    new = lax.broadcasted_iota(jnp.int32, (SUBLANES * antennas, SUBLANES * antennas), 0)
+    turn = jnp.where(new == lax.rem(old, SUBLANES) * antennas + old // SUBLANES, 1.0, 0.0).astype(square.dtype)
+
+    for g in range(groups):
+        part = landing[g].at[:, pl.ds(0, sent)]
+        pltpu.make_async_copy(part, part, recv_sem.at[g]).wait()
+
+        def expand(d, carry, g=g):
+            chan, t = d // n_tm, lax.rem(d, n_tm)
+            m = chan // 2 * n_tm + t
+            bands = []
+            for i in range(antennas):
+                band = []
+                for b in range(blocks):
+                    word = meta_ref[0, d, b * antennas + i]
+                    at, first, limit = word >> 16, (word >> 8) & 255, word & 255
+                    low = landing[g][m, at].astype(jnp.float32)
+                    high = landing[g][m, at + 1].astype(jnp.float32)
+                    piece = rotate(jnp.where(lane >= first, low, high), (limit - first) & (LANES - 1))
+                    band.append(jnp.where(lane >= limit, piece, 0.0))
+                bands.append(jnp.concatenate(band, axis=1))
+            flat = jnp.concatenate(bands, axis=0).astype(square.dtype)
+            flat = jnp.dot(turn, flat, preferred_element_type=jnp.float32).astype(square.dtype)
+            for q in range(SUBLANES):
+                square[
+                    q, pl.ds(pl.multiple_of(chan * antennas, antennas), antennas),
+                    pl.ds(pl.multiple_of(t * samples, LANES), samples),
+                ] = flat[q * antennas:(q + 1) * antennas]
+            return carry
+
+        lax.fori_loop(0, n, expand, 0)
+
+        def correlate(c, carry, g=g):
+            real, imag = square[c], square[width + c]
+            same = lax.dot_general(real, real, NT, preferred_element_type=jnp.float32)
+            same += lax.dot_general(imag, imag, NT, preferred_element_type=jnp.float32)
+            cross = lax.dot_general(imag, real, NT, preferred_element_type=jnp.float32)
+            out_ref[g * width + c, 0] = same * inverse[...]
+            out_ref[g * width + c, 1] = (cross - cross.T) * inverse[...]
+            return carry
+
+        lax.fori_loop(0, width, correlate, 0)
+
+    for g in range(groups):
+        each(lambda k, g=g: copy(g, k).wait_send())
+
+
+def packed_shards(n_chan, n_tm, voltages, flag_mask, flagged_prefix_counts):
+    parts, all_channels, antennas, samples = voltages.shape
+    n = n_chan * n_tm
+    chips = n // 2
+    channels = all_channels // n
+    width = SUBLANES // parts
+    groups = channels // width
+    blocks = samples // FLAG_BLOCK_WIDTH
+    segments = blocks * antennas
+    most = 2 * segments
+    levels = [most]
+    while levels[-1] > 8:
+        levels.append(max(8, min(levels[-1] - 1, levels[-1] * 15 // 16)))
+    levels = tuple(sorted(levels))
+    dtype = voltages.dtype
+    entries = segments + 1
+    smem = pl.BlockSpec(memory_space=pltpu.SMEM)
+    vmem = pl.BlockSpec(memory_space=pltpu.VMEM)
+    hbm = pl.BlockSpec(memory_space=pl.ANY)
+    both, table, meta, level = pl.pallas_call(
+        functools.partial(pack_kernel, n_chan, n_tm, levels),
+        out_shape=(
+            jax.ShapeDtypeStruct((2, chips, groups, entries, SUBLANES, LANES), dtype),
+            jax.ShapeDtypeStruct((n, LANES), jnp.int32),
+            jax.ShapeDtypeStruct((2, n, LANES), jnp.int32),
+            jax.ShapeDtypeStruct((1, LANES), jnp.int32),
+        ),
+        in_specs=[hbm, smem, smem],
+        out_specs=(hbm, vmem, vmem, vmem),
+        scratch_shapes=[
+            pltpu.VMEM(voltages.shape, dtype),
+            pltpu.VMEM((chips, groups, entries, SUBLANES, LANES), dtype),
+            pltpu.VMEM((chips, groups, entries, SUBLANES, LANES), dtype),
+            pltpu.VMEM((1, LANES), jnp.int32),
+            pltpu.VMEM((n, 1, LANES), jnp.int32),
+            pltpu.SMEM((3, segments), jnp.int32),
+            pltpu.SemaphoreType.DMA((n,)),
+            pltpu.SemaphoreType.DMA((n,)),
+            pltpu.SemaphoreType.DMA,
+            pltpu.SemaphoreType.DMA((chips,)),
+            pltpu.SemaphoreType.DMA,
+            pltpu.SemaphoreType.DMA((chips,)),
+            pltpu.SemaphoreType.DMA,
+        ],
+        compiler_params=pltpu.CompilerParams(
+            collective_id=0, has_side_effects=True, vmem_limit_bytes=40 * 1024 * 1024
+        ),
+    )(voltages, flag_mask, flagged_prefix_counts)
+    total_antennas, total_samples = antennas * n_chan, samples * n_tm
+
+    def unite(index, sent):
+        return pl.pallas_call(
+            functools.partial(unite_kernel, n_chan, n_tm, antennas, samples, sent),
+            out_shape=pltpu.VMEM((channels, 2, total_antennas, total_antennas), jnp.float32),
+            in_specs=[hbm, vmem, smem],
+            out_specs=vmem,
+            scratch_shapes=[pltpu.VMEM((chips, sent + 2, SUBLANES, LANES), dtype)] * groups + [
+                pltpu.VMEM((2, chips, groups, entries, SUBLANES, LANES), dtype),
+                pltpu.VMEM((groups, chips, sent, SUBLANES, LANES), dtype),
+                pltpu.VMEM((SUBLANES, total_antennas, total_samples), dtype),
+                pltpu.VMEM((total_antennas, LANES), jnp.float32),
+                pltpu.VMEM((total_antennas, total_antennas), jnp.float32),
+                pltpu.SemaphoreType.DMA,
+                pltpu.SemaphoreType.DMA((groups, chips)),
+                pltpu.SemaphoreType.DMA((groups,)),
+            ],
+            compiler_params=pltpu.CompilerParams(
+                collective_id=1 + index, has_side_effects=True, vmem_limit_bytes=48 * 1024 * 1024
+            ),
+        )
+
+    branches = [unite(index, sent) for index, sent in enumerate(levels)]
+    return lax.switch(level[0, 0], branches, both, table, meta)
+
+
+def packable(n_chan, n_tm, parts, all_channels, antennas, samples):
+    n = n_chan * n_tm
+    if n_chan % 2 or all_channels % n or SUBLANES % parts:
+        return False
+    segments = samples // FLAG_BLOCK_WIDTH * antennas
+    return all_channels // n % (SUBLANES // parts) == 0 and antennas % 16 == 0 and segments < LANES - 1
+
+
+def body(n_chan, n_tm, voltages, flag_mask, flagged_prefix_counts):
+    chosen = packed_shards if packable(n_chan, n_tm, *voltages.shape) else shards
+    return chosen(n_chan, n_tm, voltages, flag_mask, flagged_prefix_counts)
+
+
 def solution(mesh):
     placed = (P(None, None, "chan", "tm"), P("tm", "chan"), P("tm", "chan"))
     return jax.shard_map(
-        functools.partial(shards, mesh.shape["chan"], mesh.shape["tm"]),
+        functools.partial(body, mesh.shape["chan"], mesh.shape["tm"]),
         mesh=mesh,
         in_specs=placed,
         out_specs=P(("chan", "tm"), None, None, None),

time: 198 us -> 158 us (0.80); the launches traced: 198 us -> 155 us
  Pallas kernels: 193 us -> 127 us
  loops' own time: 0 us -> 19.9 us
  local copies, waits for them, and re-layouts: 4 us -> 8.14 us
    pallas_call x1 -> x2, Pallas kernels: 193 us -> 127 us  [the longest x1 105 us: packed_shards(): return lax.switch(level[0, 0], branches, both, table, meta)]
    another operation x0 -> x1, loops' own time: none -> 19.9 us  [packed_shards(): return lax.switch(level[0, 0], branches, both, table, meta)]
    unnamed x1 -> x7, local copies, waits for them, and re-layouts: 3.4 us -> 8.14 us
where the time goes in v1:
time: 158 us; the launch traced here: 155 us
  Pallas kernels  127 us (80%)
  loops' own time  19.9 us (13%)
  local copies, waits for them, and re-layouts  8.14 us (5%)
    pallas_call x1, Pallas kernels, packed_shards(): return lax.switch(level[0, 0], branches, both, table, meta)  105 us
    pallas_call x1, Pallas kernels, packed_shards(): pl.pallas_call(functools.partial(pack_kernel, n_chan, n_tm, levels), out_...  21.7 us
    another operation x1, loops' own time, packed_shards(): return lax.switch(level[0, 0], branches, both, table, meta)  19.9 us
    unnamed x7, local copies, waits for them, and re-layouts  8.14 us

profile of v1, /device:TPU:0, one launch (start us, length us, event | category | flops | bytes accessed | tf_op | source)
XLA Modules:
  0.0 155.2 jit_solution(3223989829673975944)
XLA Ops:
  0.0 0.0 copy-start
  0.0 3.4 %copy-done = bf16[2,512,16,256]{3,2,1,0:T(8,128)(2,1)S(1)} copy-done((bf16[2,512,16,256]{3,2,1,0:T(8,128)(2,1)S(1)}, bf16[2,512,16,256]{3,2,1,0:T(8,128)(2,1)}, u32[]{:S(2)}) %copy-start) | copy-done | bytes 8388632
  3.4 0.0 copy-start.1
  3.4 0.7 copy-done.1
  4.1 0.0 copy-start.2
  4.1 0.7 copy-done.2
  4.7 21.7 %shard_map.63 = (bf16[2,16,4,33,8,128]{5,4,3,2,1,0:T(8,128)(2,1)}, s32[32,128]{1,0:T(8,128)S(1)}, s32[2,32,128]{2,1,0:T(8,128)S(1)}, s32[1,128]{1,0:T(1,128)S(1)}) custom-call(bf16[2,512,16,256]{3,2,1,0:T(8,128)(2,1)S(1)} %copy-done, s32[2,16]{1,0:T(2,128)S(1)} %copy-done.1, s32[2,16]{1,0:T(2,128)S(1)} %copy-done.2), custom_call_target="tpu_custom_call" | custom-call | tf_op jit(solution)/shard_map/pallas_call | solution.py:463
  26.5 124.7 %conditional.1 = (f32[16,2,256,256]{3,2,1,0:T(8,128)S(1)}) conditional(s32[]{:T(128)} %bitcast, (bf16[2,16,4,33,8,128]{5,4,3,2,1,0:T(8,128)(2,1)}, s32[32,128]{1,0:T(8,128)S(1)}, s32[2,32,128]{2,1,0:T(8,128)S(1)}) %tuple.83, (bf16[2,16,4,33,8,128]{5,4,3,2,1,0:T(8,128)(2,1)}, s32[32,128]{1,0:T(8,128)S(1)}, ...), branch_computations={%region_0.0_spmd, %region_1.0_spmd, %region_2.0_spmd, %region_3.0_... | conditional | bytes 8 | solution.py:516
  34.8 104.8 %branch_15_fun.1 = f32[16,2,256,256]{3,2,1,0:T(8,128)S(1)} custom-call(bf16[2,16,4,33,8,128]{5,4,3,2,1,0:T(8,128)(2,1)} %get-tuple-element.233.both_ref, s32[32,128]{1,0:T(8,128)S(1)} %get-tuple-element.234.table_ref, s32[2,32,128]{2,1,0:T(8,128)S(1)} %get-tuple-element.235.meta_ref), custom_call_target="tpu_custom_call" | custom-call | tf_op jit(solution)/shard_map/cond/branch_15_fun/pallas_call | solution.py:516
  151.2 3.4 %copy.57 = f32[16,2,256,256]{3,2,1,0:T(8,128)} copy(f32[16,2,256,256]{3,2,1,0:T(8,128)S(1)} %get-tuple-element.274) | data formatting | bytes 16777216
Async XLA Ops:
  0.0 3.4 %copy-start = (bf16[2,512,16,256]{3,2,1,0:T(8,128)(2,1)S(1)}, bf16[2,512,16,256]{3,2,1,0:T(8,128)(2,1)}, u32[]{:S(2)}) copy-start(bf16[2,512,16,256]{3,2,1,0:T(8,128)(2,1)} %volt_ref.1) | copy-start | bytes 25165828
  3.4 0.7 copy-start.1
  4.1 0.7 copy-start.2
